TPU v7x, 32 devices: a whole 2x2x4 slice. The times are simulated.
32 devices in a mesh: groups: 2 (over y), gx: 16 (over z, x, core).
Axes of the slice: x: 2, y: 2, z: 4, core: 2. Of those that a mesh axis runs over, the one named last changes fastest.
Arguments:
- initial: float32 [20, 4, 256, 1024], P('groups', None, 'gx'), parts along dimension 0, may hold values from -6 to 6
- background: float32 [20, 4, 256, 1024], P('groups', None, 'gx'), parts along dimension 0, may hold values from -6.5 to 6.5
- mixing: float32 [40, 40], replicated, may hold values from -1 to 1
- diffusion: float32 [10, 4], replicated, may hold values from 0.03 to 0.2
- advection: float32 [2, 10, 4], replicated, may hold values from -0.1 to 0.1
- obs_values: float32 [4, 4096], P('groups', 'gx'), parts along dimension 0, may hold values from -6 to 6
- obs_weight: float32 [2, 4096], P('groups', 'gx'), parts along dimension 0, may hold values from 0.5 to 4
- interp_weights: float32 [8, 4096], P('groups', 'gx'), parts along dimension 0, may hold values from 0.1 to 1
- stencil_index: int32 [8, 4096], P('groups', 'gx'), parts along dimension 0, may hold values from 0 to 655359, as said below
- station_tile: int32 [4096, 2], P('gx', 'groups'), parts along dimension 1, may hold values from 0 to 15; in each aligned block of 256 rows (0 to 255, 256 to 511, ...) at most 24 rows name the same one
- counts: int32 [2, 16], P('groups', 'gx'), parts along dimension 0, may hold values from 1 to 256, 3072 in all within a row
Outputs:
- gradient: float32 [20, 4, 256, 1024], P('groups', None, 'gx'), parts along dimension 0
There are 2 independent parts, one for each index of `groups`. A program takes and returns all parts, laid end to end along the dimension named above; an argument that names none is the same for every part. Nothing has to cross between parts.
Inputs may be any that keep to these rules, and one draw needn't show every extreme that they name: `station_tile`: within the rows of one device, no tile is named more than 24 times; some tile is named exactly 24 times in some or all devices' rows. Live observations of a tile occupy its first counts slots; some tile has 256. `stencil_index`: each column holds four cells of one channel of the owner tile, a cell being (channel * 16 + row) * 1024 + column: (row, column), (row, column + 1), (row + 1, column), (row + 1, column + 1) in that order.
All inputs are finite; a program needn't handle non-finite values. No bound on the sum of `counts` on one device may be relied on, other than what follows from the above.
Results may differ from a plain program's by a relative error of at most 0.00014.
Values sent between devices are 32-bit elements; how exact they have to be, the bound alone decides.
No kernel may reach another device: no remote copies, remote signals or barrier semaphores. Data moves between devices by JAX's collectives and lax.ppermute only.
A program may use at most 64 MiB of HBM per device.

v0:
```python
import functools

import jax
import jax.numpy as jnp
from jax import lax
from jax.experimental import pallas as pl
from jax.experimental.pallas import tpu as pltpu
from jax.sharding import PartitionSpec as P

HALO = 5
LANES = 128
F32, BF16, I32 = jnp.float32, jnp.bfloat16, jnp.int32


def split3(x):
    hi = x.astype(BF16).astype(F32)
    mid = (x - hi).astype(BF16).astype(F32)
    return jnp.concatenate([hi, mid, x - hi - mid], 0).astype(BF16)


def prep_kernel(u_hbm, val, wgt, iw, cell, tile, cnt, up_hbm, dn_hbm, msg, sem, *, n, rows, cols, span):
    copies = []
    for k in range(HALO):
        copies.append(pltpu.make_async_copy(u_hbm.at[:, rows - HALO + k], up_hbm.at[k], sem.at[k]))
        copies.append(pltpu.make_async_copy(u_hbm.at[:, k], dn_hbm.at[k], sem.at[HALO + k]))
    for c in copies:
        c.start()
    held = val.shape[1]
    tgt = jnp.broadcast_to(tile[...], (held, LANES)).T[0:1, :]
    lane = lax.broadcasted_iota(I32, (1, held), 1)
    live = lane < cnt[0, 0]
    base = cell[0:1, :]
    plane = rows * cols
    chan = base // plane
    rest = base - chan * plane
    row = rest // cols
    col = rest - row * cols
    code = (chan * span + row + 4) * cols + col + tgt * plane
    feats = jnp.concatenate([val[...], wgt[...], iw[...], code.astype(F32)], 0)
    feats = split3(feats)
    dest = lax.broadcasted_iota(I32, (n, held), 0)
    hit = (tgt == dest) | ((tgt == dest + 1) & (row <= 1)) | ((tgt == dest - 1) & (row >= rows - 3))
    hit = hit & live
    tri = lax.broadcasted_iota(I32, (held, held), 0) < lax.broadcasted_iota(I32, (held, held), 1)
    hit_f = hit.astype(F32)
    rank = jnp.dot(hit_f.astype(BF16), tri.astype(F32).astype(BF16), preferred_element_type=F32)
    place = jnp.where(hit, rank, -1.0)
    total = jnp.sum(hit_f, axis=1, keepdims=True)
    slot = lax.broadcasted_iota(I32, (LANES, held), 0).astype(F32)
    sub8 = lax.broadcasted_iota(I32, (8, LANES), 0)
    lane8 = lax.broadcasted_iota(I32, (8, LANES), 1)
    for d in range(n):
        pick = (place[d : d + 1, :] == slot).astype(F32).astype(BF16)
        got = lax.dot_general(feats, pick, (((1,), (1,)), ((), ())), preferred_element_type=F32)
        got = got[0:8] + got[8:16] + got[16:24]
        got = jnp.where(sub8 == 7, got - float(d * plane), got)
        msg[d] = jnp.where((sub8 == 7) & (lane8 == LANES - 1), total[d : d + 1, 0:1], got)
    for c in copies:
        c.wait()


def main_kernel(
    edge, dif, adv, u_hbm, b_hbm, up_hbm, dn_hbm, msg_hbm, msg, mix, out_hbm,
    u0, bg, u1, u2, f1, f2, dt0, dt1, stage, tab, table, coef, mats, code_s, list_s,
    sem_u, sem_b, sem_e, sem_o, sem_m, *, n, rows, cols, chans, span,
):
    nf, nl = dif.shape
    load_u = lambda x: pltpu.make_async_copy(u_hbm.at[:, x], u0.at[HALO + x], sem_u.at[x])
    load_b = lambda x: pltpu.make_async_copy(b_hbm.at[:, x], bg.at[x], sem_b.at[x])
    store_o = lambda x: pltpu.make_async_copy(bg.at[x], out_hbm.at[:, x], sem_o.at[x])
    edges = [
        pltpu.make_async_copy(up_hbm, u0.at[pl.ds(0, HALO)], sem_e.at[0]),
        pltpu.make_async_copy(dn_hbm, u0.at[pl.ds(HALO + rows, HALO)], sem_e.at[1]),
    ]
    codes = pltpu.make_async_copy(msg_hbm.at[:, 7], code_s, sem_m)
    codes.start()
    for c in edges:
        c.start()
    for x in range(rows):
        load_u(x).start()
    for x in range(rows):
        load_b(x).start()

    for ch in range(chans):
        i, j = ch // nl, ch % nl
        c, a, b = dif[i, j], adv[0, i, j], adv[1, i, j]
        for k, v in enumerate((c + a, c - a, c + b, c - b, 1.0 - 4.0 * c)):
            coef[k, ch : ch + 1, :] = jnp.full((1, LANES), v, F32)
    mats[...] = jnp.zeros_like(mats)
    m = mix[...]
    mats[2, 0:chans, 0:chans] = m
    mt = mats[2].T[0:chans, 0:chans]
    for k, v in enumerate((m, mt)):
        hi = v.astype(BF16).astype(F32)
        lo = v - hi
        mats[k, 0:chans, 0:chans] = hi
        mats[k, 0:chans, chans : 2 * chans] = hi
        mats[k, chans : 2 * chans, 0:chans] = lo
        mats[k, chans : 2 * chans, chans : 2 * chans] = lo
    fwd = mats[0, 0 : 2 * chans, 0 : 2 * chans].astype(BF16)
    bwd = mats[1, 0 : 2 * chans, 0 : 2 * chans].astype(BF16)

    def mixed(lhs, v):
        hi = v.astype(BF16).astype(F32)
        rhs = jnp.concatenate([hi, v - hi], 0).astype(BF16)
        r = jnp.dot(lhs, rhs, preferred_element_type=F32)
        return r[0:chans] + r[chans : 2 * chans]

    lane = lax.broadcasted_iota(I32, (chans, cols), 1)

    def stencil(north, v, south, sign):
        cn, cs, ce, cw, cc = (jnp.tile(coef[k], (1, cols // LANES)) for k in range(5))
        if sign < 0:
            cn, cs, ce, cw = cs, cn, cw, ce
        east = jnp.where(lane == cols - 1, 0.0, pltpu.roll(v, cols - 1, 1))
        west = jnp.where(lane == 0, 0.0, pltpu.roll(v, 1, 1))
        return cc * v + cn * north + cs * south + ce * east + cw * west

    f1[...] = jnp.zeros_like(f1)
    f2[...] = jnp.zeros_like(f2)

    def spread(s, _):
        tab[pl.ds(s * LANES, LANES), 0:8] = msg[s].T
        return 0

    lax.fori_loop(0, n, spread, 0)
    top, bot = edge[0, 0], edge[0, 1]
    for c in edges:
        c.wait()
    for x in range(rows):
        load_u(x).wait()

    def inside(row):
        return jnp.where(row < 0, top, jnp.where(row >= rows, bot, 1.0))

    def first(k, _):
        v = u0[k + 1]
        t = jnp.tanh(v)
        r = stencil(u0[k + 2], v, u0[k], 1) + mixed(fwd, t)
        u1[k] = r * inside(k - 4)
        dt0[k] = 1.0 - t * t
        return 0

    lax.fori_loop(0, rows + 8, first, 0)

    def second(k, _):
        v = u1[k + 1]
        t = jnp.tanh(v)
        u2[k] = stencil(u1[k + 2], v, u1[k], 1) + mixed(fwd, t)
        dt1[k] = 1.0 - t * t
        return 0

    lax.fori_loop(0, rows + 6, second, 0)

    codes.wait()

    def at(code):
        q = code // cols
        y = code - q * cols
        blk = jnp.minimum(y // LANES, cols // LANES - 2)
        return q // span, q % span, pl.multiple_of(blk * LANES, LANES)

    def gather_src(s, off):
        cnt = code_s[s, LANES - 1].astype(I32)

        def one(k, p):
            code = code_s[s, k].astype(I32)
            list_s[p] = code
            ch, x, y = at(code)
            at_ch, at_y, at_p = pl.ds(ch, 1), pl.ds(y, 2 * LANES), pl.ds(p, 1)
            stage[0, at_p] = u1[x, at_ch, at_y]
            stage[1, at_p] = u1[x + 1, at_ch, at_y]
            stage[2, at_p] = u2[x - 1, at_ch, at_y]
            stage[3, at_p] = u2[x, at_ch, at_y]
            table[at_p] = tab[pl.ds(s * LANES + k, 1)]
            return p + 1

        return lax.fori_loop(0, cnt, one, off)

    count = lax.fori_loop(0, n, gather_src, 0)

    lane2 = lax.broadcasted_iota(I32, (8, 2 * LANES), 1)

    def misfits(g, _):
        p = pl.multiple_of(g * 8, 8)
        at_p = pl.ds(p, 8)
        rec = table[at_p]
        code = rec[:, 7:8].astype(I32)
        y = code - (code // cols) * cols
        l = y - jnp.minimum(y // LANES, cols // LANES - 2) * LANES
        here, nxt = lane2 == l, lane2 == l + 1
        w0 = jnp.where(here, rec[:, 3:4], 0.0) + jnp.where(nxt, rec[:, 4:5], 0.0)
        w1 = jnp.where(here, rec[:, 5:6], 0.0) + jnp.where(nxt, rec[:, 6:7], 0.0)
        w = rec[:, 2:3]
        d1 = w * (jnp.sum(w0 * stage[0, at_p] + w1 * stage[1, at_p], 1, keepdims=True) - rec[:, 0:1])
        d2 = w * (jnp.sum(w0 * stage[2, at_p] + w1 * stage[3, at_p], 1, keepdims=True) - rec[:, 1:2])
        stage[0, at_p] = d1 * w0
        stage[1, at_p] = d1 * w1
        stage[2, at_p] = d2 * w0
        stage[3, at_p] = d2 * w1
        return 0

    lax.fori_loop(0, (count + 7) // 8, misfits, 0)

    def scatter(p, _):
        ch, x, y = at(list_s[p])
        at_ch, at_y, at_p = pl.ds(ch, 1), pl.ds(y, 2 * LANES), pl.ds(p, 1)
        a = f1[x - 1, at_ch, at_y] + stage[0, at_p]
        b = f1[x, at_ch, at_y] + stage[1, at_p]
        c = f2[x - 1, at_ch, at_y] + stage[2, at_p]
        d = f2[x, at_ch, at_y] + stage[3, at_p]
        f1[x - 1, at_ch, at_y] = a
        f1[x, at_ch, at_y] = b
        f2[x - 1, at_ch, at_y] = c
        f2[x, at_ch, at_y] = d
        return 0

    lax.fori_loop(0, count, scatter, 0)

    def third(j, _):
        k = j + 2
        v = f2[k]
        r = stencil(f2[k + 1], v, f2[k - 1], -1) + dt1[k] * mixed(bwd, v) + f1[k]
        f1[k] = r * inside(j - 1)
        return 0

    lax.fori_loop(0, rows + 2, third, 0)
    for x in range(rows):
        load_b(x).wait()

    def fourth(x, _):
        k = x + 3
        v = f1[k]
        r = stencil(f1[k + 1], v, f1[k - 1], -1) + dt0[x + 4] * mixed(bwd, v)
        bg[x] = (u0[x + HALO] - bg[x]) + r
        store_o(x).start()
        return 0

    lax.fori_loop(0, rows, fourth, 0)
    for x in range(rows):
        store_o(x).wait()


def shards(
    initial, background, mixing, diffusion, advection, obs_values, obs_weight, interp_weights,
    stencil_index, station_tile, counts,
):
    fields, levels, rows, cols = initial.shape
    chans = fields * levels
    n = lax.axis_size("gx")
    held = obs_values.shape[1]
    cap = max(2, held * 3 // (2 * n))
    most = -(-3 * cap * n // 8) * 8 + 8
    span = 1 << (rows + 7).bit_length()
    u = initial.reshape(chans, rows, cols)
    b = background.reshape(chans, rows, cols)
    vmem, smem, hbm = (pl.BlockSpec(memory_space=s) for s in (pltpu.VMEM, pltpu.SMEM, pl.ANY))
    edge_shape = jax.ShapeDtypeStruct((HALO, chans, cols), F32)
    up_send, dn_send, msg = pl.pallas_call(
        functools.partial(prep_kernel, n=n, rows=rows, cols=cols, span=span),
        out_shape=(edge_shape, edge_shape, jax.ShapeDtypeStruct((n, 8, LANES), F32)),
        in_specs=[hbm, vmem, vmem, vmem, vmem, vmem, smem],
        out_specs=(hbm, hbm, vmem),
        scratch_shapes=[pltpu.SemaphoreType.DMA((2 * HALO,))],
        name="prep",
    )(u, obs_values, obs_weight, interp_weights, stencil_index, station_tile, counts)
    up = [(i, i + 1) for i in range(n - 1)]
    down = [(j, i) for i, j in up]
    from_up = lax.ppermute(up_send, "gx", up)
    from_dn = lax.ppermute(dn_send, "gx", down)
    msg = lax.all_to_all(msg, "gx", split_axis=0, concat_axis=0, tiled=True)
    me = lax.axis_index("gx")
    edge = jnp.stack([me > 0, me < n - 1]).astype(F32).reshape(1, 2)
    tile = (chans, cols)
    out = pl.pallas_call(
        functools.partial(main_kernel, n=n, rows=rows, cols=cols, chans=chans, span=span),
        out_shape=jax.ShapeDtypeStruct((chans, rows, cols), F32),
        in_specs=[smem, smem, smem, hbm, hbm, hbm, hbm, hbm, vmem, vmem],
        out_specs=hbm,
        scratch_shapes=[
            pltpu.VMEM((rows + 2 * HALO, *tile), F32),
            pltpu.VMEM((rows, *tile), F32),
            pltpu.VMEM((rows + 8, *tile), F32),
            pltpu.VMEM((rows + 6, *tile), F32),
            pltpu.VMEM((rows + 6, *tile), F32),
            pltpu.VMEM((rows + 6, *tile), F32),
            pltpu.VMEM((rows + 8, *tile), F32),
            pltpu.VMEM((rows + 6, *tile), F32),
            pltpu.VMEM((4, most, 2 * LANES), F32),
            pltpu.VMEM((n * LANES, LANES), F32),
            pltpu.VMEM((most, LANES), F32),
            pltpu.VMEM((5, chans, LANES), F32),
            pltpu.VMEM((3, LANES, LANES), F32),
            pltpu.SMEM((n, LANES), F32),
            pltpu.SMEM((most,), I32),
            pltpu.SemaphoreType.DMA((rows,)),
            pltpu.SemaphoreType.DMA((rows,)),
            pltpu.SemaphoreType.DMA((2,)),
            pltpu.SemaphoreType.DMA((rows,)),
            pltpu.SemaphoreType.DMA(()),
        ],
        compiler_params=pltpu.CompilerParams(vmem_limit_bytes=60 * 1024 * 1024),
        name="adjoint",
    )(edge, diffusion, advection, u, b, from_up, from_dn, msg, msg, mixing)
    return out.reshape(fields, levels, rows, cols)


def solution(mesh):
    placed = (
        P("groups", None, "gx", None),
        P("groups", None, "gx", None),
        P(),
        P(),
        P(),
        P("groups", "gx"),
        P("groups", "gx"),
        P("groups", "gx"),
        P("groups", "gx"),
        P("gx", "groups"),
        P("groups", "gx"),
    )
    return jax.shard_map(
        shards, mesh=mesh, in_specs=placed, out_specs=P("groups", None, "gx", None), check_vma=False
    )
```

profile of v0, /device:TPU:17, one launch (start us, length us, event | category | flops | bytes accessed | tf_op | source)
XLA Modules:
  0.0 133.7 jit_solution(1148471781487063818)
XLA Ops:
  0.0 0.0 copy-start.4
  0.0 0.0 copy-start.3
  0.7 1.5 %copy.12.tile = s32[256,1]{1,0:T(8,128)} copy(s32[256,1]{0,1:T(1,128)} %param.20) | data formatting | bytes 2048 | tf_op args[9]
  2.2 52.4 %prep.1 = (f32[5,40,1024]{2,1,0:T(8,128)}, f32[5,40,1024]{2,1,0:T(8,128)}, f32[16,8,128]{2,1,0:T(8,128)}) custom-call(f32[40,16,1024]{2,1,0:T(8,128)} %bitcast.5, f32[2,256]{1,0:T(2,128)} %val.1, f32[1,256]{1,0:T(1,128)} %wgt.1, f32[4,256]{1,0:T(4,128)} %iw.1, s32[4,256]{1,0:T(4,128)} %cell.1, s32[256,1]{1,0:T(8,128)} %copy.12.tile, s32[1,1]{1,0:T(1,128)S(6)} %copy.15.cnt), custom_call_target="tpu_custom_call" | custom-call | tf_op jit(solution)/shard_map/prep/pallas_call | solution.py:259
  54.6 3.7 %collective-permute-start = (f32[5,40,1024]{2,1,0:T(8,128)}, f32[5,40,1024]{2,1,0:T(8,128)S(1)}, u32[]{:S(2)}, u32[]{:S(2)}) collective-permute-start(f32[5,40,1024]{2,1,0:T(8,128)} %get-tuple-element.8), channel_id=1, source_target_pairs={{0,1},{1,2},{2,3},{3,4},{4,5},{5,6},{6,7},{7,8},{8,9},{9,10},{10,1... | collective-permute-start | bytes 2457608 | tf_op jit(solution)/shard_map/ppermute | solution.py:269
  58.3 1.9 %collective-permute-start.1 = (f32[5,40,1024]{2,1,0:T(8,128)}, f32[5,40,1024]{2,1,0:T(8,128)S(1)}, u32[]{:S(2)}, u32[]{:S(2)}) collective-permute-start(f32[5,40,1024]{2,1,0:T(8,128)} %get-tuple-element.9), channel_id=1, source_target_pairs={{1,0},{2,1},{3,2},{4,3},{5,4},{6,5},{7,6},{8,7},{9,8},{10,9},{11,1... | collective-permute-start | bytes 2457608 | tf_op jit(solution)/shard_map/ppermute | solution.py:270
  60.2 6.4 %all-to-all-start = ((f32[16,8,128]{2,1,0:T(8,128)}), f32[16,8,128]{2,1,0:T(8,128)S(1)}, u32[]{:S(2)}, u32[]{:S(2)}) async-start(f32[16,8,128]{2,1,0:T(8,128)} %get-tuple-element.10), calls=%async_computation | async-start | bytes 131072 | tf_op jit(solution)/shard_map/all_to_all | solution.py:271
  66.6 0.0 copy-done.4
  66.6 0.7 copy.13.dif
  67.3 0.0 copy-done.3
  67.3 0.7 copy.14.adv
  68.0 0.7 add_convert_fusion.edge
  68.6 10.4 %all-to-all-done.msg_hbm.msg = f32[16,8,128]{2,1,0:T(8,128)S(1)} async-done(((f32[16,8,128]{2,1,0:T(8,128)}), f32[16,8,128]{2,1,0:T(8,128)S(1)}, u32[]{:S(2)}, u32[]{:S(2)}) %all-to-all-start) | async-done | bytes 65568 | tf_op jit(solution)/shard_map/all_to_all | solution.py:271
  79.1 0.0 copy-start.2
  79.1 0.0 collective-permute-done.up_hbm
  79.1 0.0 copy-start
  79.1 0.0 collective-permute-done.1.dn_hbm
  79.1 0.0 copy-start.1
  79.1 0.6 copy-done.2
  79.7 0.3 copy-done
  80.0 0.2 copy-done.1
  80.3 53.4 %adjoint.1 = f32[40,16,1024]{2,1,0:T(8,128)} custom-call(f32[1,2]{1,0:T(1,128)} %add_convert_fusion.edge, f32[10,4]{1,0:T(8,128)} %copy.13.dif, f32[2,10,4]{2,1,0:T(8,128)} %copy.14.adv, f32[40,16,1024]{2,1,0:T(8,128)} %bitcast.6, f32[40,16,1024]{2,1,0:T(8,128)} %bitcast.7, f32[5,40,1024]{2,1,0:T(8,128)} %copy-done, f32[5,40,1024]{2,1,0:T(8,128)} %copy-done.1, ...), custom_call_target="tpu_custom_call" | custom-call | tf_op jit(solution)/shard_map/adjoint/pallas_call | solution.py:275
Async XLA Ops:
  0.0 66.6 %copy-start.4 = (f32[10,4]{0,1:T(4,128)S(1)}, f32[10,4]{0,1:T(4,128)}, u32[]{:S(2)}) copy-start(f32[10,4]{0,1:T(4,128)} %param.14) | copy-start | bytes 484
  0.0 67.3 %copy-start.3 = (f32[2,10,4]{1,2,0:T(4,128)S(1)}, f32[2,10,4]{1,2,0:T(4,128)}, u32[]{:S(2)}) copy-start(f32[2,10,4]{1,2,0:T(4,128)} %param.15) | copy-start | bytes 964
  54.6 24.5 %collective-permute-start = (f32[5,40,1024]{2,1,0:T(8,128)}, f32[5,40,1024]{2,1,0:T(8,128)S(1)}, u32[]{:S(2)}, u32[]{:S(2)}) collective-permute-start(f32[5,40,1024]{2,1,0:T(8,128)} %get-tuple-element.8), channel_id=1, source_target_pairs={{0,1},{1,2},{2,3},{3,4},{4,5},{5,6},{6,7},{7,8},{8,9},{9,10},{10,1... | collective-permute-start | bytes 2457608 | tf_op jit(solution)/shard_map/ppermute | solution.py:269
  58.3 20.8 %collective-permute-start.1 = (f32[5,40,1024]{2,1,0:T(8,128)}, f32[5,40,1024]{2,1,0:T(8,128)S(1)}, u32[]{:S(2)}, u32[]{:S(2)}) collective-permute-start(f32[5,40,1024]{2,1,0:T(8,128)} %get-tuple-element.9), channel_id=1, source_target_pairs={{1,0},{2,1},{3,2},{4,3},{5,4},{6,5},{7,6},{8,7},{9,8},{10,9},{11,1... | collective-permute-start | bytes 2457608 | tf_op jit(solution)/shard_map/ppermute | solution.py:270
  60.2 18.9 %all-to-all-start = ((f32[16,8,128]{2,1,0:T(8,128)}), f32[16,8,128]{2,1,0:T(8,128)S(1)}, u32[]{:S(2)}, u32[]{:S(2)}) async-start(f32[16,8,128]{2,1,0:T(8,128)} %get-tuple-element.10), calls=%async_computation | async-start | bytes 131072 | tf_op jit(solution)/shard_map/all_to_all | solution.py:271
  79.1 0.6 copy-start.2
  79.1 0.9 copy-start
  79.1 1.2 copy-start.1
where the time goes:
time: 136 us; the launch traced here: 134 us
  Pallas kernels  106 us (78%)
  starting transfers between devices  12 us (9%)
  waiting for transfers between devices  10.4 us (8%)
  local copies, waits for them, and re-layouts  4.04 us (3%)
    pallas_call x1, Pallas kernels, shards(): pl.pallas_call(functools.partial(main_kernel, n=n, rows=rows, cols=cols,...  53.4 us
    pallas_call x1, Pallas kernels, shards(): pl.pallas_call(functools.partial(prep_kernel, n=n, rows=rows, cols=cols,...  52.4 us
    all_to_all x1, waiting for transfers between devices, shards(): msg = lax.all_to_all(msg, 'gx', split_axis=0, concat_axis=0, tiled=True)  10.4 us
    all_to_all x1, starting transfers between devices, shards(): msg = lax.all_to_all(msg, 'gx', split_axis=0, concat_axis=0, tiled=True)  6.41 us
    unnamed x13, local copies, waits for them, and re-layouts  4.04 us
    ppermute x1, starting transfers between devices, shards(): from_up = lax.ppermute(up_send, 'gx', up)  3.68 us
  transfers between devices with their start and end apart: 3, of which 1 were waited for; matrix products, arithmetic and copies ran while one was open for 2% of the time, Pallas kernels for 0%

commit v1 on v0

v1 whole, which is shorter than its diff:
```python
import functools

import jax
import jax.numpy as jnp
from jax import lax
from jax.experimental import pallas as pl
from jax.experimental.pallas import tpu as pltpu
from jax.sharding import PartitionSpec as P

HALO = 5
LANES = 128
WIDE = 2 * LANES
SUB = 8
F32, BF16, I32 = jnp.float32, jnp.bfloat16, jnp.int32


def split3(x):
    hi = x.astype(BF16).astype(F32)
    mid = (x - hi).astype(BF16).astype(F32)
    return [hi, mid, x - hi - mid]


def prep_kernel(u_hbm, val, wgt, iw, cell, tile, cnt, up, dn, msg, sem, *, n, rows, cols, groups):
    copies = []
    for k in range(HALO):
        at = pl.ds(k * groups, groups)
        copies.append(pltpu.make_async_copy(u_hbm.at[:, :, rows - HALO + k], up.at[at], sem.at[k]))
        copies.append(pltpu.make_async_copy(u_hbm.at[:, :, k], dn.at[at], sem.at[HALO + k]))
    for c in copies:
        c.start()
    held = val.shape[1]
    blocks = cols // LANES
    tgt = tile[...]
    lane = lax.broadcasted_iota(I32, (1, held), 1)
    live = lane < cnt[0, 0]
    base = cell[0:1, :]
    plane = rows * cols
    chan = base // plane
    rest = base - chan * plane
    row = rest // cols
    col = rest - row * cols
    blk = jnp.minimum(col // LANES, blocks - 2)
    line = (row + 4) * groups + chan // SUB
    code = ((line * SUB + chan % SUB) * blocks + blk) * WIDE + col - blk * LANES
    step = rows * groups * SUB * blocks * WIDE
    feats = jnp.concatenate(split3(jnp.concatenate([val[...], wgt[...], iw[...], jnp.zeros((1, held), F32)], 0)), 0)
    pad = jnp.zeros((SUB - 3, held), F32)
    dest = lax.broadcasted_iota(I32, (n, held), 0)
    hit = (tgt == dest) | ((tgt == dest + 1) & (row <= 1)) | ((tgt == dest - 1) & (row >= rows - 3))
    hit = hit & live
    tri = lax.broadcasted_iota(I32, (held, held), 0) < lax.broadcasted_iota(I32, (held, held), 1)
    hit_f = hit.astype(F32)
    rank = jnp.dot(hit_f.astype(BF16), tri.astype(F32).astype(BF16), preferred_element_type=F32)
    place = jnp.where(hit, rank, -1.0)
    total = jnp.sum(hit_f, axis=1, keepdims=True)
    slot = lax.broadcasted_iota(I32, (LANES, held), 0).astype(F32)
    sub8 = lax.broadcasted_iota(I32, (SUB, LANES), 0)
    lane8 = lax.broadcasted_iota(I32, (SUB, LANES), 1)
    least = float(groups * SUB * blocks * WIDE)
    for d in range(n):
        pick = (place[d : d + 1, :] == slot).astype(F32).astype(BF16)
        code_d = (code + (tgt - d) * step).astype(F32)
        lhs = jnp.concatenate([feats, *split3(code_d), pad], 0).astype(BF16)
        got = lax.dot_general(lhs, pick, (((1,), (1,)), ((), ())), preferred_element_type=F32)
        where = jnp.maximum(got[24:25] + got[25:26] + got[26:27], least)
        got = got[0:8] + got[8:16] + got[16:24]
        got = jnp.where(sub8 == 7, where, got)
        msg[d] = jnp.where((sub8 == 7) & (lane8 == LANES - 1), total[d : d + 1, 0:1], got)
    for c in copies:
        c.wait()


def main_kernel(
    dif, adv, u_hbm, b_hbm, up_hbm, dn_hbm, msg, mix, out_hbm,
    u0, bg, u1, u2, f1, f2, dt0, dt1, stage, tab, table, coef, mats, code_v, code_s, list_s,
    sem_u, sem_b, sem_e, sem_o, sem_m, *, n, rows, cols, chans, levels,
):
    groups, blocks = chans // SUB, cols // LANES
    line = lambda ref, x: ref.at[pl.ds(x * groups, groups)]
    load_u = lambda x: pltpu.make_async_copy(u_hbm.at[:, :, x], line(u0, HALO + x), sem_u.at[x])
    load_b = lambda x: pltpu.make_async_copy(b_hbm.at[:, :, x], line(bg, x), sem_b.at[x])
    store_o = lambda x: pltpu.make_async_copy(line(bg, x), out_hbm.at[:, :, x], sem_o.at[x])
    span = HALO * groups
    edges = [
        pltpu.make_async_copy(up_hbm, u0.at[pl.ds(0, span)], sem_e.at[0]),
        pltpu.make_async_copy(dn_hbm, u0.at[pl.ds(span + rows * groups, span)], sem_e.at[1]),
    ]
    for c in edges:
        c.start()
    for x in range(rows):
        load_u(x).start()
    for x in range(rows):
        load_b(x).start()
    code_v[...] = msg[:, SUB - 1, :].astype(I32)
    codes = pltpu.make_async_copy(code_v, code_s, sem_m)
    codes.start()

    for ch in range(chans):
        i, j = ch // levels, ch % levels
        c, a, b = dif[j, i], adv[0, j, i], adv[1, j, i]
        for k, v in enumerate((c + a, c - a, c + b, c - b, 1.0 - 4.0 * c)):
            coef[k, ch : ch + 1, :] = jnp.full((1, LANES), v, F32)
    mats[2] = jnp.zeros_like(mats[2])
    m = mix[...]
    mats[2, 0:chans, 0:chans] = m
    mt = mats[2].T[0:chans, 0:chans]
    for k, v in enumerate((m, mt)):
        hi = v.astype(BF16).astype(F32)
        mats[k, 0:chans, 0:chans] = hi
        mats[k, 0:chans, chans : 2 * chans] = hi
        mats[k, 0:chans, 2 * chans : 3 * chans] = v - hi
    fwd = mats[0, 0:chans, 0 : 3 * chans].astype(BF16)
    bwd = mats[1, 0:chans, 0 : 3 * chans].astype(BF16)
    lane = lax.broadcasted_iota(I32, (chans, LANES), 1)
    zero = jnp.zeros((chans, LANES), F32)

    def get(ref, x, b):
        return ref[pl.ds(x * groups, groups), :, b * LANES : (b + 1) * LANES].reshape(chans, LANES)

    def put(ref, x, b, v):
        ref[pl.ds(x * groups, groups), :, b * LANES : (b + 1) * LANES] = v.reshape(groups, SUB, LANES)

    def mixed(lhs, parts):
        res = []
        for b in range(0, blocks, 2):
            v = jnp.concatenate(parts[b : b + 2], 1)
            hi = v.astype(BF16).astype(F32)
            rhs = jnp.concatenate([hi, v - hi, hi], 0).astype(BF16)
            r = jnp.dot(lhs, rhs, preferred_element_type=F32)
            res += [r[:, :LANES], r[:, LANES:]]
        return res

    def stencil(ref, x, parts, sign):
        kn, ks, ke, kw = (0, 1, 2, 3) if sign > 0 else (1, 0, 3, 2)
        res = []
        left = [pltpu.roll(v, LANES - 1, 1) for v in parts] + [zero]
        right = [zero] + [pltpu.roll(v, 1, 1) for v in parts]
        for b in range(blocks):
            east = jnp.where(lane == LANES - 1, left[b + 1], left[b])
            west = jnp.where(lane == 0, right[b], right[b + 1])
            r = coef[4] * parts[b] + coef[kn] * get(ref, x + 1, b) + coef[ks] * get(ref, x - 1, b)
            res.append(r + coef[ke] * east + coef[kw] * west)
        return res

    def over(count, width, body):
        def several(i, _):
            for r in range(width):
                body(i * width + r)
            return 0

        lax.fori_loop(0, count // width, several, 0)

    f1[...] = jnp.zeros_like(f1)
    f2[...] = jnp.zeros_like(f2)

    def spread(s, _):
        tab[pl.ds(s * LANES, LANES), 0:SUB] = msg[s].T
        return 0

    lax.fori_loop(0, n, spread, 0)
    me = lax.axis_index("gx")
    for c in edges:
        c.wait()
    for x in range(rows):
        load_u(x).wait()

    def first(k):
        v = [get(u0, k + 1, b) for b in range(blocks)]
        t = [jnp.tanh(p) for p in v]
        p = mixed(fwd, t)
        s = stencil(u0, k + 1, v, 1)
        for b in range(blocks):
            put(dt0, k, b, 1.0 - t[b] * t[b])
            put(u1, k, b, s[b] + p[b])

    over(rows + 8, 2, first)

    def clear(ref, x, count):
        ref[pl.ds(x * groups, count * groups)] = jnp.zeros((count * groups, SUB, cols), F32)

    @pl.when(me == 0)
    def _():
        clear(u1, 0, 4)

    @pl.when(me == n - 1)
    def _():
        clear(u1, rows + 4, 4)

    def second(k):
        v = [get(u1, k + 1, b) for b in range(blocks)]
        t = [jnp.tanh(p) for p in v]
        p = mixed(fwd, t)
        s = stencil(u1, k + 1, v, 1)
        for b in range(blocks):
            put(dt1, k, b, 1.0 - t[b] * t[b])
            put(u2, k, b, s[b] + p[b])

    over(rows + 6, 2, second)

    codes.wait()
    unroll = 4
    shift = (WIDE.bit_length() - 1, blocks.bit_length() - 1, SUB.bit_length() - 1)

    def at(code):
        q = lax.shift_right_logical(code, shift[0])
        y = pl.multiple_of(lax.shift_left(q & (blocks - 1), 7), LANES)
        q = lax.shift_right_logical(q, shift[1])
        return lax.shift_right_logical(q, shift[2]), pl.ds(q & (SUB - 1), 1), pl.ds(y, WIDE)

    def gather_src(s, off):
        cnt = code_s[s, LANES - 1]

        def some(i, _):
            for r in range(unroll):
                k = i * unroll + r
                p = off + k
                code = code_s[s, k]
                list_s[p] = code
                x, at_s, at_y = at(code)
                at_p = pl.ds(p, 1)
                stage[0, at_p] = u1[x, at_s, at_y]
                stage[1, at_p] = u1[x + groups, at_s, at_y]
                stage[2, at_p] = u2[x - groups, at_s, at_y]
                stage[3, at_p] = u2[x, at_s, at_y]
                table[at_p] = tab[pl.ds(s * LANES + k, 1)]
            return 0

        lax.fori_loop(0, lax.shift_right_logical(cnt + unroll - 1, 2), some, 0)
        return off + cnt

    count = lax.fori_loop(0, n, gather_src, 0)
    for r in range(unroll):
        list_s[count + r] = groups * SUB * blocks * WIDE

    per = 16
    lane2 = lax.broadcasted_iota(I32, (per, WIDE), 1)
    nth = lax.broadcasted_iota(I32, (per, 1), 0)

    def misfits(g, _):
        p = pl.multiple_of(g * per, per)
        at_p = pl.ds(p, per)
        rec = table[at_p]
        l = rec[:, 7:8].astype(I32) & (WIDE - 1)
        here, nxt = lane2 == l, lane2 == l + 1
        w0 = jnp.where(here, rec[:, 3:4], jnp.where(nxt, rec[:, 4:5], 0.0))
        w1 = jnp.where(here, rec[:, 5:6], jnp.where(nxt, rec[:, 6:7], 0.0))
        w = rec[:, 2:3]
        ok = p + nth < count
        d1 = w * (jnp.sum(w0 * stage[0, at_p] + w1 * stage[1, at_p], 1, keepdims=True) - rec[:, 0:1])
        d2 = w * (jnp.sum(w0 * stage[2, at_p] + w1 * stage[3, at_p], 1, keepdims=True) - rec[:, 1:2])
        stage[0, at_p] = jnp.where(ok, d1 * w0, 0.0)
        stage[1, at_p] = jnp.where(ok, d1 * w1, 0.0)
        stage[2, at_p] = jnp.where(ok, d2 * w0, 0.0)
        stage[3, at_p] = jnp.where(ok, d2 * w1, 0.0)
        return 0

    lax.fori_loop(0, lax.div(count + per - 1, per), misfits, 0)

    def scatter(i, _):
        for r in range(unroll):
            p = i * unroll + r
            x, at_s, at_y = at(list_s[p])
            at_p = pl.ds(p, 1)
            a = f1[x - groups, at_s, at_y] + stage[0, at_p]
            b = f1[x, at_s, at_y] + stage[1, at_p]
            c = f2[x - groups, at_s, at_y] + stage[2, at_p]
            d = f2[x, at_s, at_y] + stage[3, at_p]
            f1[x - groups, at_s, at_y] = a
            f1[x, at_s, at_y] = b
            f2[x - groups, at_s, at_y] = c
            f2[x, at_s, at_y] = d
        return 0

    lax.fori_loop(0, lax.shift_right_logical(count + unroll - 1, 2), scatter, 0)

    def third(j):
        k = j + 2
        v = [get(f2, k, b) for b in range(blocks)]
        p = mixed(bwd, v)
        s = stencil(f2, k, v, -1)
        for b in range(blocks):
            put(f1, k, b, (s[b] + get(f1, k, b)) + get(dt1, k, b) * p[b])

    over(rows + 2, 2, third)

    @pl.when(me == 0)
    def _():
        clear(f1, 2, 1)

    @pl.when(me == n - 1)
    def _():
        clear(f1, rows + 3, 1)

    for x in range(rows):
        load_b(x).wait()

    def fourth(x):
        k = x + 3
        v = [get(f1, k, b) for b in range(blocks)]
        p = mixed(bwd, v)
        s = stencil(f1, k, v, -1)
        for b in range(blocks):
            r = s[b] + get(dt0, x + 4, b) * p[b]
            put(bg, x, b, (get(u0, x + HALO, b) - get(bg, x, b)) + r)
        store_o(x).start()

    over(rows, 2, fourth)
    for x in range(rows):
        store_o(x).wait()


def shards(
    initial, background, mixing, diffusion, advection, obs_values, obs_weight, interp_weights,
    stencil_index, station_tile, counts,
):
    fields, levels, rows, cols = initial.shape
    chans = fields * levels
    groups = chans // SUB
    n = lax.axis_size("gx")
    held = obs_values.shape[1]
    cap = max(2, held * 3 // (2 * n))
    most = -(-3 * cap * n // 16) * 16 + 16
    u = initial.reshape(groups, SUB, rows, cols)
    b = background.reshape(groups, SUB, rows, cols)
    vmem, smem, hbm = (pl.BlockSpec(memory_space=s) for s in (pltpu.VMEM, pltpu.SMEM, pl.ANY))
    edge_shape = jax.ShapeDtypeStruct((HALO * groups, SUB, cols), F32)
    up_send, dn_send, msg = pl.pallas_call(
        functools.partial(prep_kernel, n=n, rows=rows, cols=cols, groups=groups),
        out_shape=(edge_shape, edge_shape, jax.ShapeDtypeStruct((n, SUB, LANES), F32)),
        in_specs=[hbm, vmem, vmem, vmem, vmem, vmem, smem],
        out_specs=(vmem, vmem, vmem),
        scratch_shapes=[pltpu.SemaphoreType.DMA((2 * HALO,))],
        name="prep",
    )(u, obs_values, obs_weight, interp_weights, stencil_index, station_tile.T, counts)
    up = [(i, i + 1) for i in range(n - 1)]
    down = [(j, i) for i, j in up]
    from_up = lax.ppermute(up_send, "gx", up)
    from_dn = lax.ppermute(dn_send, "gx", down)
    msg = lax.all_to_all(msg, "gx", split_axis=0, concat_axis=0, tiled=True)
    buf = lambda count: pltpu.VMEM((count * groups, SUB, cols), F32)
    out = pl.pallas_call(
        functools.partial(main_kernel, n=n, rows=rows, cols=cols, chans=chans, levels=levels),
        out_shape=jax.ShapeDtypeStruct(u.shape, F32),
        in_specs=[smem, smem, hbm, hbm, hbm, hbm, vmem, vmem],
        out_specs=hbm,
        scratch_shapes=[
            buf(rows + 2 * HALO),
            buf(rows),
            buf(rows + 8),
            buf(rows + 6),
            buf(rows + 6),
            buf(rows + 6),
            buf(rows + 8),
            buf(rows + 6),
            pltpu.VMEM((4, most, WIDE), F32),
            pltpu.VMEM((n * LANES, LANES), F32),
            pltpu.VMEM((most, LANES), F32),
            pltpu.VMEM((5, chans, LANES), F32),
            pltpu.VMEM((3, LANES, LANES), F32),
            pltpu.VMEM((n, LANES), I32),
            pltpu.SMEM((n, LANES), I32),
            pltpu.SMEM((most,), I32),
            pltpu.SemaphoreType.DMA((rows,)),
            pltpu.SemaphoreType.DMA((rows,)),
            pltpu.SemaphoreType.DMA((2,)),
            pltpu.SemaphoreType.DMA((rows,)),
            pltpu.SemaphoreType.DMA(()),
        ],
        compiler_params=pltpu.CompilerParams(vmem_limit_bytes=56 * 1024 * 1024),
        name="adjoint",
    )(diffusion.T, advection.transpose(0, 2, 1), u, b, from_up, from_dn, msg, mixing)
    return out.reshape(fields, levels, rows, cols)


def solution(mesh):
    placed = (
        P("groups", None, "gx", None),
        P("groups", None, "gx", None),
        P(),
        P(),
        P(),
        P("groups", "gx"),
        P("groups", "gx"),
        P("groups", "gx"),
        P("groups", "gx"),
        P("gx", "groups"),
        P("groups", "gx"),
    )
    return jax.shard_map(
        shards, mesh=mesh, in_specs=placed, out_specs=P("groups", None, "gx", None), check_vma=False
    )
```

time: 136 us -> 62.6 us (0.46)
  the two profiles are of different devices: /device:TPU:17 before, /device:TPU:12 now
where the time goes in v1:
time: 62.6 us; the launch traced here: 61.8 us
  Pallas kernels  35.7 us (57%)
  blocking collectives  17.8 us (28%)
  starting transfers between devices  6.46 us (10%)
  local copies, waits for them, and re-layouts  1.16 us (2%)
  between operations  0.69 us (1%)
    pallas_call x1, Pallas kernels, shards(): pl.pallas_call(functools.partial(main_kernel, n=n, rows=rows, cols=cols,...  32 us
    all_to_all x1, blocking collectives, shards(): msg = lax.all_to_all(msg, 'gx', split_axis=0, concat_axis=0, tiled=True)  17.8 us
    ppermute x1, starting transfers between devices, shards(): from_dn = lax.ppermute(dn_send, 'gx', down)  4.54 us
    pallas_call x1, Pallas kernels, shards(): pl.pallas_call(functools.partial(prep_kernel, n=n, rows=rows, cols=cols,...  3.67 us
    ppermute x1, starting transfers between devices, shards(): from_up = lax.ppermute(up_send, 'gx', up)  1.92 us
  transfers between devices with their start and end apart: 2, of which 0 were waited for; matrix products, arithmetic and copies ran while one was open for 0% of the time, Pallas kernels for 0%

profile of v1, /device:TPU:12, one launch (start us, length us, event | category | flops | bytes accessed | tf_op | source)
XLA Modules:
  0.0 61.8 jit_solution(5316150327489754169)
XLA Ops:
  0.7 3.7 %prep.1 = (f32[25,8,1024]{2,1,0:T(8,128)}, f32[25,8,1024]{2,1,0:T(8,128)}, f32[16,8,128]{2,1,0:T(8,128)}) custom-call(f32[5,8,16,1024]{3,2,1,0:T(8,128)} %bitcast.6, f32[2,256]{1,0:T(2,128)} %val.1, f32[1,256]{1,0:T(1,128)} %wgt.1, f32[4,256]{1,0:T(4,128)} %iw.1, s32[4,256]{1,0:T(4,128)} %cell.1, s32[1,256]{1,0:T(1,128)} %bitcast.11, s32[1,1]{1,0:T(1,128)S(6)} %copy.12.cnt), custom_call_target="tpu_custom_call" | custom-call | tf_op jit(solution)/shard_map/prep/pallas_call | solution.py:327
  4.3 1.9 %collective-permute-start = (f32[25,8,1024]{2,1,0:T(8,128)}, f32[25,8,1024]{2,1,0:T(8,128)S(1)}, u32[]{:S(2)}, u32[]{:S(2)}) collective-permute-start(f32[25,8,1024]{2,1,0:T(8,128)} %get-tuple-element.8), channel_id=1, source_target_pairs={{0,1},{1,2},{2,3},{3,4},{4,5},{5,6},{6,7},{7,8},{8,9},{9,10},{10,1... | collective-permute-start | bytes 2457608 | tf_op jit(solution)/shard_map/ppermute | solution.py:337
  6.3 4.5 %collective-permute-start.1 = (f32[25,8,1024]{2,1,0:T(8,128)}, f32[25,8,1024]{2,1,0:T(8,128)S(1)}, u32[]{:S(2)}, u32[]{:S(2)}) collective-permute-start(f32[25,8,1024]{2,1,0:T(8,128)} %get-tuple-element.9), channel_id=1, source_target_pairs={{1,0},{2,1},{3,2},{4,3},{5,4},{6,5},{7,6},{8,7},{9,8},{10,9},{11,1... | collective-permute-start | bytes 2457608 | tf_op jit(solution)/shard_map/ppermute | solution.py:338
  10.8 17.8 %all_to_all.5.msg = f32[16,8,128]{2,1,0:T(8,128)} all-to-all(f32[16,8,128]{2,1,0:T(8,128)} %get-tuple-element.10), channel_id=1, replica_groups=mesh['groups'=2,'gx'=16] {'gx'}, dimensions={0} | all-to-all | bytes 131072 | tf_op jit(solution)/shard_map/all_to_all | solution.py:339
  28.6 0.0 collective-permute-done.up_hbm
  28.6 0.0 copy-start
  28.6 0.0 collective-permute-done.1.dn_hbm
  28.7 0.0 copy-start.1
  28.7 0.9 %copy-done = f32[25,8,1024]{2,1,0:T(8,128)} copy-done((f32[25,8,1024]{2,1,0:T(8,128)}, f32[25,8,1024]{2,1,0:T(8,128)S(1)}, u32[]{:S(2)}) %copy-start) | copy-done | bytes 819224
  29.6 0.3 copy-done.1
  29.8 32.0 %adjoint.1 = f32[5,8,16,1024]{3,2,1,0:T(8,128)} custom-call(f32[4,10]{1,0:T(4,128)} %bitcast.10, f32[2,4,10]{2,1,0:T(4,128)} %bitcast.9, f32[5,8,16,1024]{3,2,1,0:T(8,128)} %bitcast.7, f32[5,8,16,1024]{3,2,1,0:T(8,128)} %bitcast.8, f32[25,8,1024]{2,1,0:T(8,128)} %copy-done, f32[25,8,1024]{2,1,0:T(8,128)} %copy-done.1, f32[16,8,128]{2,1,0:T(8,128)} %all_to_all.5.msg, ...), custom_call_target="tpu_custom_call" | custom-call | tf_op jit(solution)/shard_map/adjoint/pallas_call | solution.py:341
Async XLA Ops:
  4.3 24.3 %collective-permute-start = (f32[25,8,1024]{2,1,0:T(8,128)}, f32[25,8,1024]{2,1,0:T(8,128)S(1)}, u32[]{:S(2)}, u32[]{:S(2)}) collective-permute-start(f32[25,8,1024]{2,1,0:T(8,128)} %get-tuple-element.8), channel_id=1, source_target_pairs={{0,1},{1,2},{2,3},{3,4},{4,5},{5,6},{6,7},{7,8},{8,9},{9,10},{10,1... | collective-permute-start | bytes 2457608 | tf_op jit(solution)/shard_map/ppermute | solution.py:337
  6.3 22.4 %collective-permute-start.1 = (f32[25,8,1024]{2,1,0:T(8,128)}, f32[25,8,1024]{2,1,0:T(8,128)S(1)}, u32[]{:S(2)}, u32[]{:S(2)}) collective-permute-start(f32[25,8,1024]{2,1,0:T(8,128)} %get-tuple-element.9), channel_id=1, source_target_pairs={{1,0},{2,1},{3,2},{4,3},{5,4},{6,5},{7,6},{8,7},{9,8},{10,9},{11,1... | collective-permute-start | bytes 2457608 | tf_op jit(solution)/shard_map/ppermute | solution.py:338
  28.6 0.9 %copy-start = (f32[25,8,1024]{2,1,0:T(8,128)}, f32[25,8,1024]{2,1,0:T(8,128)S(1)}, u32[]{:S(2)}) copy-start(f32[25,8,1024]{2,1,0:T(8,128)S(1)} %collective-permute-done.up_hbm) | copy-start | bytes 2457604
  28.7 1.2 %copy-start.1 = (f32[25,8,1024]{2,1,0:T(8,128)}, f32[25,8,1024]{2,1,0:T(8,128)S(1)}, u32[]{:S(2)}) copy-start(f32[25,8,1024]{2,1,0:T(8,128)S(1)} %collective-permute-done.1.dn_hbm) | copy-start | bytes 2457604

commit v2 on v1

v2 whole, which is shorter than its diff:
```python
import functools

import jax
import jax.numpy as jnp
from jax import lax
from jax.experimental import pallas as pl
from jax.experimental.pallas import tpu as pltpu
from jax.sharding import PartitionSpec as P

HALO = 5
LANES = 128
WIDE = 2 * LANES
SUB = 8
F32, BF16, I32 = jnp.float32, jnp.bfloat16, jnp.int32


def split3(x):
    hi = x.astype(BF16).astype(F32)
    mid = (x - hi).astype(BF16).astype(F32)
    return [hi, mid, x - hi - mid]


def edges_kernel(u_hbm, up, dn, sem, *, rows, groups):
    copies = []
    for k in range(HALO):
        at = pl.ds(k * groups, groups)
        copies.append(pltpu.make_async_copy(u_hbm.at[:, :, rows - HALO + k], up.at[at], sem.at[k]))
        copies.append(pltpu.make_async_copy(u_hbm.at[:, :, k], dn.at[at], sem.at[HALO + k]))
    for c in copies:
        c.start()
    for c in copies:
        c.wait()


def bucket_kernel(val, wgt, iw, cell, tile, cnt, msg, *, n, rows, cols, groups):
    held = val.shape[1]
    blocks = cols // LANES
    tgt = tile[...]
    lane = lax.broadcasted_iota(I32, (1, held), 1)
    live = lane < cnt[0, 0]
    base = cell[0:1, :]
    plane = rows * cols
    chan = base // plane
    rest = base - chan * plane
    row = rest // cols
    col = rest - row * cols
    blk = jnp.minimum(col // LANES, blocks - 2)
    line = (row + 4) * groups + chan // SUB
    code = ((line * SUB + chan % SUB) * blocks + blk) * WIDE + col - blk * LANES
    step = rows * groups * SUB * blocks * WIDE
    feats = jnp.concatenate(split3(jnp.concatenate([val[...], wgt[...], iw[...], jnp.zeros((1, held), F32)], 0)), 0)
    pad = jnp.zeros((SUB - 3, held), F32)
    dest = lax.broadcasted_iota(I32, (n, held), 0)
    hit = (tgt == dest) | ((tgt == dest + 1) & (row <= 1)) | ((tgt == dest - 1) & (row >= rows - 3))
    hit = hit & live
    tri = lax.broadcasted_iota(I32, (held, held), 0) < lax.broadcasted_iota(I32, (held, held), 1)
    hit_f = hit.astype(F32)
    rank = jnp.dot(hit_f.astype(BF16), tri.astype(F32).astype(BF16), preferred_element_type=F32)
    place = jnp.where(hit, rank, -1.0)
    total = jnp.sum(hit_f, axis=1, keepdims=True)
    slot = lax.broadcasted_iota(I32, (LANES, held), 0).astype(F32)
    sub8 = lax.broadcasted_iota(I32, (SUB, LANES), 0)
    lane8 = lax.broadcasted_iota(I32, (SUB, LANES), 1)
    least = float(groups * SUB * blocks * WIDE)
    for d in range(n):
        pick = (place[d : d + 1, :] == slot).astype(F32).astype(BF16)
        code_d = (code + (tgt - d) * step).astype(F32)
        lhs = jnp.concatenate([feats, *split3(code_d), pad], 0).astype(BF16)
        got = lax.dot_general(lhs, pick, (((1,), (1,)), ((), ())), preferred_element_type=F32)
        where = jnp.maximum(got[24:25] + got[25:26] + got[26:27], least)
        got = got[0:8] + got[8:16] + got[16:24]
        got = jnp.where(sub8 == 7, where, got)
        msg[d] = jnp.where((sub8 == 7) & (lane8 == LANES - 1), total[d : d + 1, 0:1], got)


class Dense:
    def __init__(self, coef, chans, cols):
        self.coef, self.chans, self.cols = coef, chans, cols
        self.groups, self.blocks = chans // SUB, cols // LANES

    def get(self, ref, x, b):
        v = ref[pl.ds(x * self.groups, self.groups), :, b * LANES : (b + 1) * LANES]
        return v.reshape(self.chans, LANES)

    def row(self, ref, x):
        return [self.get(ref, x, b) for b in range(self.blocks)]

    def put(self, ref, x, b, v):
        at = pl.ds(x * self.groups, self.groups)
        ref[at, :, b * LANES : (b + 1) * LANES] = v.reshape(self.groups, SUB, LANES)

    def mixed(self, lhs, parts):
        res = []
        for b in range(0, self.blocks, 2):
            v = jnp.concatenate(parts[b : b + 2], 1)
            hi = v.astype(BF16).astype(F32)
            rhs = jnp.concatenate([hi, v - hi, hi], 0).astype(BF16)
            r = jnp.dot(lhs, rhs, preferred_element_type=F32)
            res += [r[:, :LANES], r[:, LANES:]]
        return res

    def stencil(self, ref, x, parts, sign):
        coef = self.coef
        lane = lax.broadcasted_iota(I32, (self.chans, LANES), 1)
        zero = jnp.zeros((self.chans, LANES), F32)
        kn, ks, ke, kw = (0, 1, 2, 3) if sign > 0 else (1, 0, 3, 2)
        res = []
        left = [pltpu.roll(v, LANES - 1, 1) for v in parts] + [zero]
        right = [zero] + [pltpu.roll(v, 1, 1) for v in parts]
        for b in range(self.blocks):
            east = jnp.where(lane == LANES - 1, left[b + 1], left[b])
            west = jnp.where(lane == 0, right[b], right[b + 1])
            r = coef[4] * parts[b] + coef[kn] * self.get(ref, x + 1, b) + coef[ks] * self.get(ref, x - 1, b)
            res.append(r + coef[ke] * east + coef[kw] * west)
        return res

    def advance(self, src, x, lhs, dst, slope, y):
        v = self.row(src, x)
        t = [jnp.tanh(p) for p in v]
        p = self.mixed(lhs, t)
        s = self.stencil(src, x, v, 1)
        for b in range(self.blocks):
            self.put(slope, y, b, 1.0 - t[b] * t[b])
            self.put(dst, y, b, s[b] + p[b])


def over(count, bodies):
    def several(i, _):
        for body in bodies:
            body(i)
        return 0

    lax.fori_loop(0, count, several, 0)


def weights(mats, k, chans):
    return mats[k, 0:chans, 0 : 3 * chans].astype(BF16)


def scatter_coefficients(coef, mats, dif, adv, mix, chans, levels):
    for ch in range(chans):
        i, j = ch // levels, ch % levels
        c, a, b = dif[j, i], adv[0, j, i], adv[1, j, i]
        for k, v in enumerate((c + a, c - a, c + b, c - b, 1.0 - 4.0 * c)):
            coef[k, ch : ch + 1, :] = jnp.full((1, LANES), v, F32)
    mats[2] = jnp.zeros((LANES, LANES), F32)
    m = mix[...]
    mats[2, 0:chans, 0:chans] = m
    mt = mats[2].T[0:chans, 0:chans]
    for k, v in enumerate((m, mt)):
        hi = v.astype(BF16).astype(F32)
        mats[k, 0:chans, 0:chans] = hi
        mats[k, 0:chans, chans : 2 * chans] = hi
        mats[k, 0:chans, 2 * chans : 3 * chans] = v - hi


def inner_kernel(
    dif, adv, u_hbm, b_hbm, mix, u1_out, u2_out, dt0_out, dt1_out, base_out, coef, mats,
    u0, base, u1, u2, dt0, dt1, sem_u, sem_b, sem_o, *, rows, cols, chans, levels,
):
    dense = Dense(coef, chans, cols)
    groups = dense.groups
    line = lambda ref, x: ref.at[pl.ds(x * groups, groups)]
    load_u = [pltpu.make_async_copy(u_hbm.at[:, :, x], line(u0, x), sem_u.at[x]) for x in range(rows)]
    load_b = [pltpu.make_async_copy(b_hbm.at[:, :, x], line(base, x), sem_b.at[x]) for x in range(rows)]
    for c in load_u + load_b:
        c.start()
    scatter_coefficients(coef, mats, dif, adv, mix, chans, levels)
    fwd = weights(mats, 0, chans)
    give = lambda ref, out, x, k: pltpu.make_async_copy(line(ref, x), line(out, x), sem_o.at[k, x])
    for c in load_u:
        c.wait()

    def step(off):
        def body(i):
            x = off + i
            dense.advance(u0, x + 1, fwd, u1, dt0, x)
            give(u1, u1_out, x, 0).start()
            give(dt0, dt0_out, x, 1).start()

        return body

    def step2(off):
        def body(i):
            x = off + i
            dense.advance(u1, x + 1, fwd, u2, dt1, x)
            give(u2, u2_out, x, 2).start()
            give(dt1, dt1_out, x, 3).start()

        return body

    half, half2 = (rows - 2) // 2, (rows - 4) // 2
    over(half, [step(0), step(half)])
    over(half2, [step2(0), step2(half2)])
    for c in load_b:
        c.wait()

    def departure(x):
        for b in range(dense.blocks):
            dense.put(base, x, b, dense.get(u0, x, b) - dense.get(base, x, b))
        give(base, base_out, x, 4).start()

    over(rows, [departure])
    for x in range(rows - 2):
        give(u1, u1_out, x, 0).wait()
        give(dt0, dt0_out, x, 1).wait()
    for x in range(rows - 4):
        give(u2, u2_out, x, 2).wait()
        give(dt1, dt1_out, x, 3).wait()
    for x in range(rows):
        give(base, base_out, x, 4).wait()


def main_kernel(
    up_hbm, dn_hbm, msg, u_hbm, u1_in, u2_in, dt0_in, dt1_in, base_in, coef, mats,
    out_hbm, u0, base, u1, u2, f1, f2, dt0, dt1,
    stage, tab, table, code_v, code_s, list_s, sem_e, sem_i, sem_o, sem_m, *, n, rows, cols, chans,
):
    dense = Dense(coef, chans, cols)
    groups, blocks = dense.groups, dense.blocks
    line = lambda ref, x: ref.at[pl.ds(x * groups, groups)]
    store_o = lambda x: pltpu.make_async_copy(line(base, x), out_hbm.at[:, :, x], sem_o.at[x])
    span = HALO * groups
    edges = [
        pltpu.make_async_copy(up_hbm, u0.at[pl.ds(0, span)], sem_e.at[0]),
        pltpu.make_async_copy(dn_hbm, u0.at[pl.ds(span + rows * groups, span)], sem_e.at[1]),
    ]
    for k, x in enumerate((0, 1, rows - 2, rows - 1)):
        edges.append(pltpu.make_async_copy(u_hbm.at[:, :, x], line(u0, HALO + x), sem_e.at[2 + k]))
    bulk = lambda src, ref, x, count, k: pltpu.make_async_copy(
        src, ref.at[pl.ds(x * groups, count * groups)], sem_i.at[k]
    )
    early = [bulk(u1_in, u1, 5, rows - 2, 0), bulk(u2_in, u2, 5, rows - 4, 1)]
    late = [bulk(dt1_in, dt1, 5, rows - 4, 2), bulk(dt0_in, dt0, 5, rows - 2, 3), bulk(base_in, base, 0, rows, 4)]
    for c in edges + early + late:
        c.start()
    code_v[...] = msg[:, SUB - 1, :].astype(I32)
    codes = pltpu.make_async_copy(code_v, code_s, sem_m)
    codes.start()
    fwd, bwd = weights(mats, 0, chans), weights(mats, 1, chans)

    def spread(i):
        for r in range(4):
            s = i * 4 + r
            tab[pl.ds(s * LANES, LANES), 0:SUB] = msg[s].T

    over(n // 4, [spread])
    f1[...] = jnp.zeros_like(f1)
    f2[...] = jnp.zeros_like(f2)
    me = lax.axis_index("gx")
    for c in edges:
        c.wait()

    def clear(ref, x, count):
        ref[pl.ds(x * groups, count * groups)] = jnp.zeros((count * groups, SUB, cols), F32)

    step = lambda off: lambda i: dense.advance(u0, off + 1 + i, fwd, u1, dt0, off + i)
    over(5, [step(0), step(rows + 3)])

    @pl.when(me == 0)
    def _():
        clear(u1, 0, 4)

    @pl.when(me == n - 1)
    def _():
        clear(u1, rows + 4, 4)

    for c in early:
        c.wait()

    step2 = lambda off: lambda i: dense.advance(u1, off + 1 + i, fwd, u2, dt1, off + i)
    over(5, [step2(0), step2(rows + 1)])

    codes.wait()
    unroll = 4
    shift = (WIDE.bit_length() - 1, blocks.bit_length() - 1, SUB.bit_length() - 1)

    def at(code):
        q = lax.shift_right_logical(code, shift[0])
        y = pl.multiple_of(lax.shift_left(q & (blocks - 1), 7), LANES)
        q = lax.shift_right_logical(q, shift[1])
        return lax.shift_right_logical(q, shift[2]), pl.ds(q & (SUB - 1), 1), pl.ds(y, WIDE)

    def gather_src(s, off):
        cnt = code_s[s, LANES - 1]

        def some(i, _):
            for r in range(unroll):
                k = i * unroll + r
                p = off + k
                code = code_s[s, k]
                list_s[p] = code
                x, at_s, at_y = at(code)
                at_p = pl.ds(p, 1)
                stage[0, at_p] = u1[x, at_s, at_y]
                stage[1, at_p] = u1[x + groups, at_s, at_y]
                stage[2, at_p] = u2[x - groups, at_s, at_y]
                stage[3, at_p] = u2[x, at_s, at_y]
                table[at_p] = tab[pl.ds(s * LANES + k, 1)]
            return 0

        lax.fori_loop(0, lax.shift_right_logical(cnt + unroll - 1, 2), some, 0)
        return off + cnt

    count = lax.fori_loop(0, n, gather_src, 0)
    for r in range(unroll):
        list_s[count + r] = groups * SUB * blocks * WIDE

    per = 64
    lane1 = lax.broadcasted_iota(I32, (per, LANES), 1)
    nth = lax.broadcasted_iota(I32, (per, LANES), 0)

    def misfits(g, _):
        p = pl.multiple_of(g * per, per)
        at_p = pl.ds(p, per)
        rec = table[at_p]
        wide = lambda k: jnp.broadcast_to(rec[:, k : k + 1], (per, LANES))
        l = wide(7).astype(I32) & (WIDE - 1)
        iw = [wide(k) for k in range(3, 7)]
        ws = []
        for h in range(2):
            here, nxt = lane1 == l - h * LANES, lane1 == l + (1 - h * LANES)
            ws.append([jnp.where(here, iw[k], jnp.where(nxt, iw[k + 1], 0.0)) for k in (0, 2)])
        w = jnp.where(p + nth < count, wide(2), 0.0)
        for t in range(2):
            q = 0.0
            for k in range(2):
                for h in range(2):
                    q = q + ws[h][k] * stage[2 * t + k, at_p, h * LANES : (h + 1) * LANES]
            d = jnp.broadcast_to(jnp.sum(q, 1, keepdims=True), (per, LANES)) - wide(t)
            d = jnp.where(w > 0.0, w * d, 0.0)
            for k in range(2):
                for h in range(2):
                    stage[2 * t + k, at_p, h * LANES : (h + 1) * LANES] = d * ws[h][k]
        return 0

    lax.fori_loop(0, lax.div(count + per - 1, per), misfits, 0)

    def scatter(i, _):
        for r in range(unroll):
            p = i * unroll + r
            x, at_s, at_y = at(list_s[p])
            at_p = pl.ds(p, 1)
            a = f1[x - groups, at_s, at_y] + stage[0, at_p]
            b = f1[x, at_s, at_y] + stage[1, at_p]
            c = f2[x - groups, at_s, at_y] + stage[2, at_p]
            d = f2[x, at_s, at_y] + stage[3, at_p]
            f1[x - groups, at_s, at_y] = a
            f1[x, at_s, at_y] = b
            f2[x - groups, at_s, at_y] = c
            f2[x, at_s, at_y] = d
        return 0

    lax.fori_loop(0, lax.shift_right_logical(count + unroll - 1, 2), scatter, 0)

    def third(off):
        def body(i):
            k = off + i
            v = dense.row(f2, k)
            p = dense.mixed(bwd, v)
            s = dense.stencil(f2, k, v, -1)
            for b in range(blocks):
                dense.put(f1, k, b, (s[b] + dense.get(f1, k, b)) + dense.get(dt1, k, b) * p[b])

        return body

    for c in late:
        c.wait()
    half = (rows + 2) // 2
    over(half, [third(2), third(2 + half)])

    @pl.when(me == 0)
    def _():
        clear(f1, 2, 1)

    @pl.when(me == n - 1)
    def _():
        clear(f1, rows + 3, 1)

    def fourth(off):
        def body(i):
            x = off + i
            k = x + 3
            v = dense.row(f1, k)
            p = dense.mixed(bwd, v)
            s = dense.stencil(f1, k, v, -1)
            for b in range(blocks):
                r = s[b] + dense.get(dt0, x + 4, b) * p[b]
                dense.put(base, x, b, dense.get(base, x, b) + r)
            store_o(x).start()

        return body

    over(rows // 2, [fourth(0), fourth(rows // 2)])
    for x in range(rows):
        store_o(x).wait()


def shards(
    initial, background, mixing, diffusion, advection, obs_values, obs_weight, interp_weights,
    stencil_index, station_tile, counts,
):
    fields, levels, rows, cols = initial.shape
    chans = fields * levels
    groups = chans // SUB
    n = lax.axis_size("gx")
    held = obs_values.shape[1]
    cap = max(2, held * 3 // (2 * n))
    most = -(-3 * cap * n // 64) * 64 + 64
    in_hbm = lambda x: pltpu.with_memory_space_constraint(x, pltpu.HBM)
    u = in_hbm(initial.reshape(groups, SUB, rows, cols))
    b = in_hbm(background.reshape(groups, SUB, rows, cols))
    vmem, smem, hbm = (pl.BlockSpec(memory_space=s) for s in (pltpu.VMEM, pltpu.SMEM, pltpu.HBM))
    anywhere = pl.BlockSpec(memory_space=pl.ANY)
    buf = lambda count: pltpu.VMEM((count * groups, SUB, cols), F32)
    shape = lambda count: jax.ShapeDtypeStruct((count * groups, SUB, cols), F32)
    up_send, dn_send = pl.pallas_call(
        functools.partial(edges_kernel, rows=rows, groups=groups),
        out_shape=(shape(HALO), shape(HALO)),
        in_specs=[hbm],
        out_specs=(vmem, vmem),
        scratch_shapes=[pltpu.SemaphoreType.DMA((2 * HALO,))],
        compiler_params=pltpu.CompilerParams(vmem_limit_bytes=16 << 20),
        name="edges",
    )(u)
    up = [(i, i + 1) for i in range(n - 1)]
    down = [(j, i) for i, j in up]
    from_up = lax.ppermute(up_send, "gx", up)
    from_dn = lax.ppermute(dn_send, "gx", down)
    msg = pl.pallas_call(
        functools.partial(bucket_kernel, n=n, rows=rows, cols=cols, groups=groups),
        out_shape=jax.ShapeDtypeStruct((n, SUB, LANES), F32),
        in_specs=[vmem, vmem, vmem, vmem, vmem, smem],
        out_specs=vmem,
        compiler_params=pltpu.CompilerParams(vmem_limit_bytes=16 << 20),
        name="bucket",
    )(obs_values, obs_weight, interp_weights, stencil_index, station_tile.T, counts)
    msg = lax.all_to_all(msg, "gx", split_axis=0, concat_axis=0, tiled=True)
    dma = pltpu.SemaphoreType.DMA
    ready = pl.pallas_call(
        functools.partial(inner_kernel, rows=rows, cols=cols, chans=chans, levels=levels),
        out_shape=(
            *[pltpu.HBM(((rows - k) * groups, SUB, cols), F32) for k in (2, 4, 2, 4, 0)],
            jax.ShapeDtypeStruct((5, chans, LANES), F32),
            jax.ShapeDtypeStruct((3, LANES, LANES), F32),
        ),
        in_specs=[smem, smem, hbm, hbm, vmem],
        out_specs=(*[hbm] * 5, vmem, vmem),
        scratch_shapes=[buf(rows - k) for k in (0, 0, 2, 4, 2, 4)]
        + [dma((rows,)), dma((rows,)), dma((5, rows))],
        compiler_params=pltpu.CompilerParams(vmem_limit_bytes=24 << 20),
        name="inner",
    )(diffusion.T, advection.transpose(0, 2, 1), u, b, mixing)
    out = pl.pallas_call(
        functools.partial(main_kernel, n=n, rows=rows, cols=cols, chans=chans),
        out_shape=jax.ShapeDtypeStruct(u.shape, F32),
        in_specs=[anywhere, anywhere, vmem, *[hbm] * 6, vmem, vmem],
        out_specs=hbm,
        scratch_shapes=[buf(rows + k) for k in (2 * HALO, 0, 8, 6, 6, 6, 8, 6)]
        + [
            pltpu.VMEM((4, most, WIDE), F32),
            pltpu.VMEM((n * LANES, LANES), F32),
            pltpu.VMEM((most, LANES), F32),
            pltpu.VMEM((n, LANES), I32),
            pltpu.SMEM((n, LANES), I32),
            pltpu.SMEM((most,), I32),
            dma((6,)),
            dma((5,)),
            dma((rows,)),
            dma(()),
        ],
        compiler_params=pltpu.CompilerParams(vmem_limit_bytes=48 << 20),
        name="adjoint",
    )(from_up, from_dn, msg, u, *map(in_hbm, ready[:5]), *ready[5:])
    return out.reshape(fields, levels, rows, cols)


def solution(mesh):
    placed = (
        P("groups", None, "gx", None),
        P("groups", None, "gx", None),
        P(),
        P(),
        P(),
        P("groups", "gx"),
        P("groups", "gx"),
        P("groups", "gx"),
        P("groups", "gx"),
        P("gx", "groups"),
        P("groups", "gx"),
    )
    return jax.shard_map(
        shards, mesh=mesh, in_specs=placed, out_specs=P("groups", None, "gx", None), check_vma=False
    )
```

time: 62.6 us -> 47.6 us (0.76)
  the two profiles are of different devices: /device:TPU:12 before, /device:TPU:17 now
where the time goes in v2:
time: 47.6 us; the launch traced here: 47.2 us
  Pallas kernels  33 us (69%)
  starting transfers between devices  12 us (25%)
  waiting for transfers between devices  1.43 us (3%)
  between operations  0.78 us (2%)
    pallas_call x1, Pallas kernels, shards(): pl.pallas_call(functools.partial(main_kernel, n=n, rows=rows, cols=cols,...  19.9 us
    pallas_call x1, Pallas kernels, shards(): pl.pallas_call(functools.partial(inner_kernel, rows=rows, cols=cols, chan...  9.04 us
    all_to_all x1, starting transfers between devices, shards(): msg = lax.all_to_all(msg, 'gx', split_axis=0, concat_axis=0, tiled=True)  6.4 us
    ppermute x1, starting transfers between devices, shards(): from_up = lax.ppermute(up_send, 'gx', up)  3.68 us
    pallas_call x1, Pallas kernels, shards(): pl.pallas_call(functools.partial(edges_kernel, rows=rows, groups=groups),...  2.7 us
    ppermute x1, starting transfers between devices, shards(): from_dn = lax.ppermute(dn_send, 'gx', down)  1.92 us
    all_to_all x1, waiting for transfers between devices, shards(): msg = lax.all_to_all(msg, 'gx', split_axis=0, concat_axis=0, tiled=True)  1.42 us
    pallas_call x1, Pallas kernels, shards(): pl.pallas_call(functools.partial(bucket_kernel, n=n, rows=rows, cols=cols...  1.27 us
  transfers between devices with their start and end apart: 3, of which 1 were waited for; matrix products, arithmetic and copies ran while one was open for 0% of the time, Pallas kernels for 22%

profile of v2, /device:TPU:17, one launch (start us, length us, event | category | flops | bytes accessed | tf_op | source)
XLA Modules:
  0.0 47.2 jit_solution(11856906558322820407)
XLA Ops:
  0.0 0.0 copy-start.7
  0.0 0.0 copy-start.3
  0.0 0.0 copy-start.2
  0.0 0.0 copy-start.6
  0.0 0.0 copy-start.5
  0.0 0.0 copy-start.1
  0.0 0.0 copy-start.4
  0.0 0.0 copy-start
  0.1 2.7 %edges.1 = (f32[25,8,1024]{2,1,0:T(8,128)}, f32[25,8,1024]{2,1,0:T(8,128)S(1)}) custom-call(f32[5,8,16,1024]{3,2,1,0:T(8,128)} %bitcast.9), custom_call_target="tpu_custom_call" | custom-call | tf_op jit(solution)/shard_map/edges/pallas_call | solution.py:417
  2.8 3.7 %collective-permute-start = (f32[25,8,1024]{2,1,0:T(8,128)}, f32[25,8,1024]{2,1,0:T(8,128)S(1)}, u32[]{:S(2)}, u32[]{:S(2)}) collective-permute-start(f32[25,8,1024]{2,1,0:T(8,128)} %get-tuple-element.14), channel_id=1, source_target_pairs={{0,1},{1,2},{2,3},{3,4},{4,5},{5,6},{6,7},{7,8},{8,9},{9,10},{10,1... | collective-permute-start | bytes 2457608 | tf_op jit(solution)/shard_map/ppermute | solution.py:428
  6.5 1.9 %collective-permute-start.1 = (f32[25,8,1024]{2,1,0:T(8,128)S(1)}, f32[25,8,1024]{2,1,0:T(8,128)S(1)}, u32[]{:S(2)}, u32[]{:S(2)}) collective-permute-start(f32[25,8,1024]{2,1,0:T(8,128)S(1)} %get-tuple-element.15), channel_id=1, source_target_pairs={{1,0},{2,1},{3,2},{4,3},{5,4},{6,5},{7,6},{8,7},{9,8},{10,9},{11,1... | collective-permute-start | bytes 2457608 | tf_op jit(solution)/shard_map/ppermute | solution.py:429
  9.0 0.0 copy-done.7
  9.0 0.0 copy-done.3
  9.1 0.0 copy-done.2
  9.1 0.0 copy-done.6
  9.1 0.0 copy-done.5
  9.1 1.3 %bucket.1 = f32[16,8,128]{2,1,0:T(8,128)} custom-call(f32[2,256]{1,0:T(2,128)S(1)} %copy-done.5, f32[1,256]{1,0:T(1,128)S(1)} %copy-done.6, f32[4,256]{1,0:T(4,128)S(1)} %copy-done.2, s32[4,256]{1,0:T(4,128)S(1)} %copy-done.3, s32[1,256]{1,0:T(1,128)S(1)} %bitcast.8, s32[1,1]{1,0:T(1,128)S(6)} %copy.12.cnt), custom_call_target="tpu_custom_call" | custom-call | tf_op jit(solution)/shard_map/bucket/pallas_call | solution.py:430
  10.4 6.4 %all-to-all-start = ((f32[16,8,128]{2,1,0:T(8,128)}), f32[16,8,128]{2,1,0:T(8,128)S(1)}, u32[]{:S(2)}, u32[]{:S(2)}) async-start(f32[16,8,128]{2,1,0:T(8,128)} %bucket.1), calls=%async_computation | async-start | bytes 131072 | tf_op jit(solution)/shard_map/all_to_all | solution.py:438
  16.8 0.0 copy-done.1
  16.8 0.0 copy-done.4
  16.8 0.0 copy-done
  16.8 9.0 %inner.1 = (f32[70,8,1024]{2,1,0:T(8,128)}, f32[60,8,1024]{2,1,0:T(8,128)}, f32[70,8,1024]{2,1,0:T(8,128)}, f32[60,8,1024]{2,1,0:T(8,128)}, f32[80,8,1024]{2,1,0...) custom-call(f32[4,10]{1,0:T(4,128)S(1)} %bitcast.7, f32[2,4,10]{2,1,0:T(4,128)S(1)} %bitcast.6, ...), custom_call_target="tpu_custom_call" | custom-call | tf_op jit(solution)/shard_map/inner/pallas_call | solution.py:440
  25.8 1.4 %all-to-all-done.msg = f32[16,8,128]{2,1,0:T(8,128)S(1)} async-done(((f32[16,8,128]{2,1,0:T(8,128)}), f32[16,8,128]{2,1,0:T(8,128)S(1)}, u32[]{:S(2)}, u32[]{:S(2)}) %all-to-all-start) | async-done | bytes 65568 | tf_op jit(solution)/shard_map/all_to_all | solution.py:438
  27.3 0.0 collective-permute-done.up_hbm
  27.3 0.0 collective-permute-done.1.dn_hbm
  27.3 19.9 %adjoint.1 = f32[5,8,16,1024]{3,2,1,0:T(8,128)} custom-call(f32[25,8,1024]{2,1,0:T(8,128)S(1)} %collective-permute-done.up_hbm, f32[25,8,1024]{2,1,0:T(8,128)S(1)} %collective-permute-done.1.dn_hbm, f32[16,8,128]{2,1,0:T(8,128)S(1)} %all-to-all-done.msg, f32[5,8,16,1024]{3,2,1,0:T(8,128)} %bitcast.11, f32[70,8,1024]{2,1,0:T(8,128)} %get-tuple-element.16.u1_in, ...), custom_call_target="tpu_custom_call" | custom-call | tf_op jit(solution)/shard_map/adjoint/pallas_call | solution.py:454
Async XLA Ops:
  0.0 9.0 %copy-start.7 = (s32[256,1]{0,1:T(1,128)S(1)}, s32[256,1]{0,1:T(1,128)}, u32[]{:S(2)}) copy-start(s32[256,1]{0,1:T(1,128)} %param.20) | copy-start | bytes 3076
  0.0 9.0 %copy-start.3 = (s32[4,256]{1,0:T(4,128)S(1)}, s32[4,256]{1,0:T(4,128)}, u32[]{:S(2)}) copy-start(s32[4,256]{1,0:T(4,128)} %cell.1) | copy-start | bytes 12292
  0.0 9.1 %copy-start.2 = (f32[4,256]{1,0:T(4,128)S(1)}, f32[4,256]{1,0:T(4,128)}, u32[]{:S(2)}) copy-start(f32[4,256]{1,0:T(4,128)} %iw.1) | copy-start | bytes 12292
  0.0 9.1 %copy-start.6 = (f32[1,256]{1,0:T(1,128)S(1)}, f32[1,256]{1,0:T(1,128)}, u32[]{:S(2)}) copy-start(f32[1,256]{1,0:T(1,128)} %wgt.1) | copy-start | bytes 3076
  0.0 9.1 %copy-start.5 = (f32[2,256]{1,0:T(2,128)S(1)}, f32[2,256]{1,0:T(2,128)}, u32[]{:S(2)}) copy-start(f32[2,256]{1,0:T(2,128)} %val.1) | copy-start | bytes 6148
  0.0 16.7 %copy-start.1 = (f32[2,10,4]{1,2,0:T(4,128)S(1)}, f32[2,10,4]{1,2,0:T(4,128)}, u32[]{:S(2)}) copy-start(f32[2,10,4]{1,2,0:T(4,128)} %param.15) | copy-start | bytes 964
  0.0 16.7 %copy-start.4 = (f32[10,4]{0,1:T(4,128)S(1)}, f32[10,4]{0,1:T(4,128)}, u32[]{:S(2)}) copy-start(f32[10,4]{0,1:T(4,128)} %param.14) | copy-start | bytes 484
  0.0 16.7 %copy-start = (f32[40,40]{1,0:T(8,128)S(1)}, f32[40,40]{1,0:T(8,128)}, u32[]{:S(2)}) copy-start(f32[40,40]{1,0:T(8,128)} %mix.1) | copy-start | bytes 19204
  2.8 24.5 %collective-permute-start = (f32[25,8,1024]{2,1,0:T(8,128)}, f32[25,8,1024]{2,1,0:T(8,128)S(1)}, u32[]{:S(2)}, u32[]{:S(2)}) collective-permute-start(f32[25,8,1024]{2,1,0:T(8,128)} %get-tuple-element.14), channel_id=1, source_target_pairs={{0,1},{1,2},{2,3},{3,4},{4,5},{5,6},{6,7},{7,8},{8,9},{9,10},{10,1... | collective-permute-start | bytes 2457608 | tf_op jit(solution)/shard_map/ppermute | solution.py:428
  6.5 20.8 %collective-permute-start.1 = (f32[25,8,1024]{2,1,0:T(8,128)S(1)}, f32[25,8,1024]{2,1,0:T(8,128)S(1)}, u32[]{:S(2)}, u32[]{:S(2)}) collective-permute-start(f32[25,8,1024]{2,1,0:T(8,128)S(1)} %get-tuple-element.15), channel_id=1, source_target_pairs={{1,0},{2,1},{3,2},{4,3},{5,4},{6,5},{7,6},{8,7},{9,8},{10,9},{11,1... | collective-permute-start | bytes 2457608 | tf_op jit(solution)/shard_map/ppermute | solution.py:429
  10.4 16.9 %all-to-all-start = ((f32[16,8,128]{2,1,0:T(8,128)}), f32[16,8,128]{2,1,0:T(8,128)S(1)}, u32[]{:S(2)}, u32[]{:S(2)}) async-start(f32[16,8,128]{2,1,0:T(8,128)} %bucket.1), calls=%async_computation | async-start | bytes 131072 | tf_op jit(solution)/shard_map/all_to_all | solution.py:438
